TPU v7x, 512 devices: a whole 4x4x16 slice. The times are simulated.
512 devices in a mesh: seq: 64 (over z, x_lo, core), tp: 8 (over x_hi, y).
Axes of the slice: x: 4 (x_hi: 2, x_lo: 2; x = x_hi * 2 + x_lo), y: 4, z: 16, core: 2. Of those that a mesh axis runs over, the one named last changes fastest.
Arguments:
- tokens: bfloat16 [32768, 3584], P(('seq', 'tp')), may hold values from -6 to 6
- pre_gain: float32 [3584], replicated, may hold values from 0.25 to 1.75
- post_gain: float32 [3584], replicated, may hold values from 0.25 to 1.75
- w_query: bfloat16 [3584, 4096], P('seq', 'tp'), may hold values from -0.09375 to 0.09375
- key_matrix: bfloat16 [3584, 2048], P('seq', 'tp'), may hold values from -0.09375 to 0.09375
- value_matrix: bfloat16 [3584, 2048], P('seq', 'tp'), may hold values from -0.09375 to 0.09375
- w_out: bfloat16 [4096, 3584], P('tp', 'seq'), may hold values from -0.09375 to 0.09375
Outputs:
- block_out: bfloat16 [32768, 3584], P(('seq', 'tp'))
All inputs are finite; a program needn't handle non-finite values.
Results may differ from a plain program's by a relative error of at most 0.014.
Values may be sent and summed in bfloat16 or wider, within the bound.
No kernel may reach another device: no remote copies, remote signals or barrier semaphores. Data moves between devices by JAX's collectives and lax.ppermute only.
A program may use at most 64 MiB of HBM per device.

v0:
```python
import jax
import jax.numpy as jnp
from jax import lax
from jax.sharding import Mesh
from jax.sharding import PartitionSpec as P

HEAD_SIZE = 256
BLOCK_TOKENS = 512
SEQ = ("seq_0", "seq_1", "seq_2")
TP = ("tp_0", "tp_1")
SEQ_TP = ("seq_0", "seq_1", "seq_2", "tp_0", "tp_1")


def side_by_side(arrays, axis, dim, along):
    widths = [a.shape[along] for a in arrays]
    both = jnp.concatenate(arrays, axis=along)
    result = lax.all_gather(both, axis, axis=dim, tiled=True)
    return tuple(jnp.split(result, [sum(widths[:k]) for k in range(1, len(widths))], axis=along))


def sent_to_all(x, axis):
    length = lax.axis_size(axis)
    return lax.all_to_all(jnp.broadcast_to(x[None], (length, *x.shape)), axis, 0, 0, tiled=True)


def joined_along(pieces, dim):
    lengths = list(pieces.shape[1:])
    lengths[dim] *= pieces.shape[0]
    return jnp.moveaxis(pieces, 0, dim).reshape(lengths)


def gather_axes(x, axes, dim):
    far, near = axes
    pieces = sent_to_all(sent_to_all(x, far), near)
    return joined_along(pieces.swapaxes(0, 1).reshape(-1, *x.shape), dim)


def from_behind(x, axis, by):
    length = lax.axis_size(axis)
    pairs = [(i, i + by) for i in range(length) if 0 <= i + by < length]
    return lax.ppermute(x, axis, pairs)


def reduced_to_own(pieces, axes, turns):
    lengths = [lax.axis_size(a) for a in axes]
    pieces = pieces.reshape(*lengths, *pieces.shape[1:])
    pieces = pieces.transpose(*turns, *range(len(axes), pieces.ndim))
    pieces = pieces.reshape(-1, *pieces.shape[len(axes) :])
    for k in turns:
        pieces = lax.psum_scatter(pieces, axes[k], scatter_dimension=0, tiled=True)
    return pieces[0]


def cut_along(x, dim, length):
    before, after = (x.shape[:dim], x.shape[dim + 1 :])
    return jnp.moveaxis(x.reshape(*before, length, -1, *after), dim, 0)


def sum_by_axis(x, axes, turns, dim):
    length = lax.axis_size(axes)
    return reduced_to_own(cut_along(x, dim, length), axes, turns)


def root_norm(values, gain):
    values = values.astype(jnp.float32)
    return values * lax.rsqrt(jnp.mean(values * values, axis=-1, keepdims=True) + 1e-06) * gain


def rotate_halves(values, token_positions):
    row_count = values.shape[0]
    shaped = values.reshape(row_count, -1, HEAD_SIZE)
    half_dim = HEAD_SIZE // 2
    freq = 10000.0 ** (-(jnp.arange(half_dim).astype(jnp.float32) * 2.0 / HEAD_SIZE))
    angle = token_positions[:, None] * freq[None, :]
    cosine = jnp.cos(angle)[:, None, :]
    sine_part = jnp.sin(angle)[:, None, :]
    first = shaped[..., :half_dim]
    second = shaped[..., half_dim:]
    turned = jnp.concatenate(
        [first * cosine - second * sine_part, second * cosine + first * sine_part], axis=-1
    )
    return turned.reshape(row_count, -1)


def attend(query_rows, keys_now, vals_now, keys_prior, vals_prior, offset_pos):
    length = query_rows.shape[0]
    kv_heads = keys_now.shape[1] // HEAD_SIZE
    repeat_heads = query_rows.shape[1] // (HEAD_SIZE * kv_heads)
    query_grouped = query_rows.reshape(length, kv_heads, repeat_heads, HEAD_SIZE)
    key_current = jnp.concatenate([keys_prior, keys_now], axis=0).reshape(
        2 * length, kv_heads, HEAD_SIZE
    )
    value_current = jnp.concatenate([vals_prior, vals_now], axis=0).reshape(
        2 * length, kv_heads, HEAD_SIZE
    )
    attention_scores = jnp.einsum(
        "cwap,bwp->wacb", query_grouped, key_current, preferred_element_type=jnp.float32
    )
    query_idx = jnp.arange(length)[:, None]
    key_idx = jnp.arange(2 * length)[None, :]
    key_pos = offset_pos - length + key_idx
    allowed = (key_idx > query_idx) & (key_idx <= query_idx + length) & (key_pos >= 0)
    weights = jnp.where(allowed, jnp.exp(attention_scores), 0.0)
    denominator = jnp.sum(weights, axis=-1)
    weight_narrow = weights.astype(jnp.bfloat16)
    reduced_output = jnp.einsum(
        "bpqu,ubm->qbpm", weight_narrow, value_current, preferred_element_type=jnp.float32
    )
    attended = reduced_output / jnp.transpose(denominator, (2, 0, 1))[..., None]
    return attended.astype(jnp.bfloat16).reshape(length, -1)


def local(tokens, pre_gain, post_gain, w_query, key_matrix, value_matrix, w_out):
    normalized_input = root_norm(tokens, pre_gain).astype(jnp.bfloat16)
    query_cols = w_query.shape[1]
    key_cols = key_matrix.shape[1]
    full_query, full_key, full_value = side_by_side((w_query, key_matrix, value_matrix), SEQ, 0, 1)
    out_full = gather_axes(w_out, (("seq_0", "seq_1"), "seq_2"), 1)
    piece = lax.all_gather(normalized_input, TP, axis=0, tiled=True)
    joined = jnp.concatenate(
        [
            jnp.dot(piece, full_query, preferred_element_type=jnp.float32),
            jnp.dot(piece, full_key, preferred_element_type=jnp.float32),
            jnp.dot(piece, full_value, preferred_element_type=jnp.float32),
        ],
        axis=1,
    )
    raw_q = joined[:, :query_cols]
    raw_k = joined[:, query_cols : query_cols + key_cols]
    raw_v = joined[:, query_cols + key_cols :]
    offset_pos = lax.axis_index(SEQ) * BLOCK_TOKENS
    token_positions = (offset_pos + jnp.arange(BLOCK_TOKENS)).astype(jnp.float32)
    query_rows = (rotate_halves(raw_q, token_positions) * HEAD_SIZE ** (-0.5)).astype(jnp.bfloat16)
    keys_now = rotate_halves(raw_k, token_positions).astype(jnp.bfloat16)
    vals_now = raw_v.astype(jnp.bfloat16)
    keys_prior, vals_prior = from_behind((keys_now, vals_now), SEQ, 1)
    attended = attend(query_rows, keys_now, vals_now, keys_prior, vals_prior, offset_pos)
    partial_value = jnp.dot(attended, out_full, preferred_element_type=jnp.float32)
    own_rows = sum_by_axis(partial_value.astype(jnp.bfloat16), TP, (1, 0), 0).astype(jnp.float32)
    mixed = root_norm(own_rows, post_gain)
    return (tokens.astype(jnp.float32) + mixed).astype(jnp.bfloat16)


def solution(mesh):
    finer = Mesh(mesh.devices.reshape(16, 2, 2, 2, 4), ("seq_0", "seq_1", "seq_2", "tp_0", "tp_1"))
    in_specs = (P(SEQ_TP, None), P(), P(), P(SEQ, TP), P(SEQ, TP), P(SEQ, TP), P(TP, SEQ))
    out_specs = P(SEQ_TP, None)
    return jax.shard_map(local, mesh=finer, in_specs=in_specs, out_specs=out_specs, check_vma=False)
```

profile of v0, /device:TPU:1, one launch (start us, length us, event | category | flops | bytes accessed | tf_op | source)
XLA Modules:
  0.0 357.4 jit_solution(15433159561457681202)
XLA Ops:
  6.5 1.2 fusion.29
  7.8 2.0 fusion.31
  9.8 1.5 pad_maximum_fusion
  11.4 2.2 broadcast_in_dim.12
  13.6 16.9 %all-to-all-start = ((bf16[32,512,56]{1,2,0:T(8,128)(2,1)}), bf16[32,512,56]{1,2,0:T(8,128)(2,1)S(1)}, u32[]{:S(2)}, u32[]{:S(2)}) async-start(bf16[32,512,56]{1,2,0:T(8,128)(2,1)} %broadcast_in_dim.12), calls=%async_computation | async-start | bytes 3670016 | tf_op jit(solution)/shard_map/all_to_all | solution.py:23
  32.1 84.1 %all-to-all-done = bf16[32,512,56]{1,2,0:T(8,128)(2,1)S(1)} async-done(((bf16[32,512,56]{1,2,0:T(8,128)(2,1)}), bf16[32,512,56]{1,2,0:T(8,128)(2,1)S(1)}, u32[]{:S(2)}, u32[]{:S(2)}) %all-to-all-start) | async-done | bytes 1835040 | tf_op jit(solution)/shard_map/all_to_all | solution.py:23
  116.4 7.6 %all_to_all.10 = bf16[2,32,512,56]{2,3,1,0:T(8,128)(2,1)S(1)} all-to-all(bf16[2,32,512,56]{2,3,1,0:T(8,128)(2,1)S(1)} %broadcast_in_dim.13), channel_id=1, replica_groups=mesh['seq_0'=16,'seq_1'=2,'seq_2'=2,'tp_0'=2,'tp_1'=4] {'seq_2'}, dimensions={0} | all-to-all | bytes 7340032 | tf_op jit(solution)/shard_map/all_to_all | solution.py:23
  124.0 2.3 copy.26
  126.4 109.0 %all-gather.5.cloned.1.call-done = bf16[3584,1024]{1,0:T(8,128)(2,1)} async-done(((bf16[56,1024]{1,0:T(8,128)(2,1)}), bf16[3584,1024]{1,0:T(8,128)(2,1)}) %all-gather.5.cloned.1.call-update) | async-done | bytes 7340048 | tf_op jit(solution)/shard_map/all_gather | solution.py:17
  235.4 4.6 %fusion.21 = bf16[512,256]{1,0:T(8,128)(2,1)} fusion(bf16[512,3584]{1,0:T(8,128)(2,1)} %all-gather.3.cloned.1.call-done, bf16[3584,1024]{1,0:T(8,128)(2,1)} %all-gather.5.cloned.1.call-done), kind=kOutput, calls=%fused_computation.23 | convolution fusion | flops 939655168 | bytes 5767168 | tf_op jit(solution)/shard_map/dot_general | solution.py:124
  240.0 3.2 collective-permute-start
  243.2 3.2 fusion.18
  246.4 1.2 fusion.45
  247.6 2.1 fusion.2
  250.0 2.3 collective-permute-start.1
  252.7 2.8 collective-permute-done.1
  255.5 2.1 fusion
  257.6 2.2 divide_convert_fusion
  259.8 2.1 convolution_convert_fusion
  261.9 2.2 copy.27
  264.2 50.4 %reduce-scatter.3.cloned.1.call-done = bf16[2,64,3584]{2,1,0:T(8,128)(2,1)} async-done(((bf16[8,64,3584]{2,1,0:T(8,128)(2,1)}), bf16[2,64,3584]{2,1,0:T(8,128)(2,1)}) %reduce-scatter.3.cloned.1.call-update) | async-done | bytes 917520 | tf_op jit(solution)/shard_map/reduce_scatter | solution.py:50
  314.7 33.0 %reduce-scatter.5.cloned.1.call-done = bf16[1,64,3584]{2,1,0:T(8,128)(2,1)} async-done(((bf16[2,64,3584]{2,1,0:T(8,128)(2,1)}), bf16[1,64,3584]{2,1,0:T(8,128)(2,1)}) %reduce-scatter.5.cloned.1.call-update) | async-done | bytes 458768 | tf_op jit(solution)/shard_map/reduce_scatter | solution.py:50
  347.6 1.2 fusion.27
  348.9 2.0 fusion.32
  (34 shorter events, 2.5 us)
Async XLA Ops:
  6.5 119.8 %all-gather.3.cloned.1.call-start = ((), (), s32[]{:S(2)}) async-start(), calls=%async_computation.4 | async-start | bytes 4128768 | tf_op jit(solution)/shard_map/all_gather | solution.py:119
  9.8 225.6 %all-gather.5.cloned.1.call-start = ((), (), s32[]{:S(2)}) async-start(), calls=%async_computation.5 | async-start | bytes 7454720 | tf_op jit(solution)/shard_map/all_gather | solution.py:17
  13.6 102.6 %all-to-all-start = ((bf16[32,512,56]{1,2,0:T(8,128)(2,1)}), bf16[32,512,56]{1,2,0:T(8,128)(2,1)S(1)}, u32[]{:S(2)}, u32[]{:S(2)}) async-start(bf16[32,512,56]{1,2,0:T(8,128)(2,1)} %broadcast_in_dim.12), calls=%async_computation | async-start | bytes 3670016 | tf_op jit(solution)/shard_map/all_to_all | solution.py:23
  30.5 284.1 %reduce-scatter.3.cloned.1.call-start = ((), (), s32[]{:S(2)}) async-start(), calls=%async_computation.6 | async-start | bytes 4587520 | tf_op jit(solution)/shard_map/reduce_scatter | solution.py:50
  235.4 7.8 %copy-start.3 = (bf16[3584,1024]{1,0:T(8,128)(2,1)S(1)}, bf16[3584,1024]{1,0:T(8,128)(2,1)}, u32[]{:S(2)}) copy-start(bf16[3584,1024]{1,0:T(8,128)(2,1)} %all-gather.5.cloned.1.call-done) | copy-start | bytes 22020100
  240.0 7.7 %copy-start.4 = (bf16[512,3584]{1,0:T(8,128)(2,1)S(1)}, bf16[512,3584]{1,0:T(8,128)(2,1)}, u32[]{:S(2)}) copy-start(bf16[512,3584]{1,0:T(8,128)(2,1)} %all-gather.3.cloned.1.call-done) | copy-start | bytes 11010052
  240.0 17.6 %collective-permute-start = (bf16[512,256]{1,0:T(8,128)(2,1)}, bf16[512,256]{1,0:T(8,128)(2,1)}, u32[]{:S(2)}, u32[]{:S(2)}) collective-permute-start(bf16[512,256]{1,0:T(8,128)(2,1)} %fusion.21), channel_id=1, source_target_pairs={{0,8},{8,16},{16,24},{24,32},{32,40},{40,48},{48,56},{56,64},{64,7... | collective-permute-start | bytes 786440 | tf_op jit(solution)/shard_map/ppermute | solution.py:41
  250.0 5.4 %collective-permute-start.1 = (bf16[512,256]{0,1:T(8,128)(2,1)S(1)}, bf16[512,256]{0,1:T(8,128)(2,1)}, u32[]{:S(2)}, u32[]{:S(2)}) collective-permute-start(bf16[512,256]{0,1:T(8,128)(2,1)S(1)} %maximum_bitcast_fusion.4), channel_id=1, source_target_pairs={{0,8},{8,16},{16,24},{24,32},{32,40},{40,48},{48,56},{56,64},{64,7... | collective-permute-start | bytes 786440 | tf_op jit(solution)/shard_map/ppermute | solution.py:41
  257.6 2.2 copy-start.1
  264.1 84.7 %copy-start = (bf16[64,3584]{1,0:T(8,128)(2,1)S(1)}, bf16[64,3584]{1,0:T(8,128)(2,1)}, u32[]{:S(2)}) copy-start(bf16[64,3584]{1,0:T(8,128)(2,1)} %param.7) | copy-start | bytes 1376260
  264.1 84.8 %copy-start.2 = (f32[3584]{0:T(1024)S(1)}, f32[3584]{0:T(1024)}, u32[]{:S(2)}) copy-start(f32[3584]{0:T(1024)} %param.9) | copy-start | bytes 43012
  264.1 83.5 %reduce-scatter.5.cloned.1.call-start = ((), (), s32[]{:S(2)}) async-start(), calls=%async_computation.7 | async-start | bytes 1376256 | tf_op jit(solution)/shard_map/reduce_scatter | solution.py:50
Sparse Core Ops, SparseCore 0:
  10.5 95.6 all-gather.2
  108.3 127.0 all-gather.4
  264.3 50.3 reduce-scatter.2
  317.3 30.3 reduce-scatter.4
where the time goes:
time: 358 us; the launch traced here: 357 us
  waiting for transfers between devices  279 us (78%)
  starting transfers between devices  22.6 us (6%)
  matrix products  16.3 us (5%)
  between operations  13.4 us (4%)
  other arithmetic  10.7 us (3%)
  blocking collectives  7.6 us (2%)
  local copies, waits for them, and re-layouts  7.42 us (2%)
    all_gather x1, waiting for transfers between devices, side_by_side(): result = lax.all_gather(both, axis, axis=dim, tiled=True)  109 us
    all_to_all x1, waiting for transfers between devices, sent_to_all(): lax.all_to_all(jnp.broadcast_to(x[None], (length, *x.shape)), axis, 0, 0,...  84.1 us
    reduce_scatter x2, waiting for transfers between devices, reduced_to_own(): pieces = lax.psum_scatter(pieces, axes[k], scatter_dimension=0, tiled=True)  83.4 us
    all_to_all x1, starting transfers between devices, sent_to_all(): lax.all_to_all(jnp.broadcast_to(x[None], (length, *x.shape)), axis, 0, 0,...  16.9 us
    all_to_all x1, blocking collectives, sent_to_all(): lax.all_to_all(jnp.broadcast_to(x[None], (length, *x.shape)), axis, 0, 0,...  7.6 us
  transfers between devices with their start and end apart: 7, of which 5 were waited for; matrix products, arithmetic and copies ran while one was open for 5% of the time, Pallas kernels for 0%

commit v1 on v0

--- a/solution.py
+++ b/solution.py
@@ -11,54 +11,27 @@
 SEQ_TP = ("seq_0", "seq_1", "seq_2", "tp_0", "tp_1")
 
 
-def side_by_side(arrays, axis, dim, along):
-    widths = [a.shape[along] for a in arrays]
-    both = jnp.concatenate(arrays, axis=along)
-    result = lax.all_gather(both, axis, axis=dim, tiled=True)
-    return tuple(jnp.split(result, [sum(widths[:k]) for k in range(1, len(widths))], axis=along))
+def to_every_tp(x):
+    length = lax.axis_size(TP)
+    return lax.all_to_all(jnp.broadcast_to(x[None], (length, *x.shape)), TP, 0, 0, tiled=True)
 
 
-def sent_to_all(x, axis):
-    length = lax.axis_size(axis)
-    return lax.all_to_all(jnp.broadcast_to(x[None], (length, *x.shape)), axis, 0, 0, tiled=True)
-
-
-def joined_along(pieces, dim):
-    lengths = list(pieces.shape[1:])
-    lengths[dim] *= pieces.shape[0]
-    return jnp.moveaxis(pieces, 0, dim).reshape(lengths)
-
-
-def gather_axes(x, axes, dim):
-    far, near = axes
-    pieces = sent_to_all(sent_to_all(x, far), near)
-    return joined_along(pieces.swapaxes(0, 1).reshape(-1, *x.shape), dim)
+def weights_of_heads(slab):
+    pair = ("seq_1", "seq_2")
+    first = lax.ppermute(slab, pair, [(1, 0), (0, 2), (3, 1), (2, 3)])
+    second = lax.ppermute(slab, pair, [(1, 2), (2, 1)])
+    chip, core = lax.axis_index("seq_1"), lax.axis_index("seq_2")
+    same = chip == core
+    upper = jnp.where(same, jnp.where(core == 0, slab, first), jnp.where(core == 0, first, second))
+    lower = jnp.where(same, jnp.where(core == 0, first, slab), jnp.where(core == 0, second, first))
+    mine = jnp.concatenate([upper, lower], axis=0)
+    return lax.all_gather(mine, ("seq_0", "seq_2"), axis=0, tiled=True)
 
 
 def from_behind(x, axis, by):
     length = lax.axis_size(axis)
     pairs = [(i, i + by) for i in range(length) if 0 <= i + by < length]
     return lax.ppermute(x, axis, pairs)
-
-
-def reduced_to_own(pieces, axes, turns):
-    lengths = [lax.axis_size(a) for a in axes]
-    pieces = pieces.reshape(*lengths, *pieces.shape[1:])
-    pieces = pieces.transpose(*turns, *range(len(axes), pieces.ndim))
-    pieces = pieces.reshape(-1, *pieces.shape[len(axes) :])
-    for k in turns:
-        pieces = lax.psum_scatter(pieces, axes[k], scatter_dimension=0, tiled=True)
-    return pieces[0]
-
-
-def cut_along(x, dim, length):
-    before, after = (x.shape[:dim], x.shape[dim + 1 :])
-    return jnp.moveaxis(x.reshape(*before, length, -1, *after), dim, 0)
-
-
-def sum_by_axis(x, axes, turns, dim):
-    length = lax.axis_size(axes)
-    return reduced_to_own(cut_along(x, dim, length), axes, turns)
 
 
 def root_norm(values, gain):
@@ -114,17 +87,11 @@
     normalized_input = root_norm(tokens, pre_gain).astype(jnp.bfloat16)
     query_cols = w_query.shape[1]
     key_cols = key_matrix.shape[1]
-    full_query, full_key, full_value = side_by_side((w_query, key_matrix, value_matrix), SEQ, 0, 1)
-    out_full = gather_axes(w_out, (("seq_0", "seq_1"), "seq_2"), 1)
-    piece = lax.all_gather(normalized_input, TP, axis=0, tiled=True)
-    joined = jnp.concatenate(
-        [
-            jnp.dot(piece, full_query, preferred_element_type=jnp.float32),
-            jnp.dot(piece, full_key, preferred_element_type=jnp.float32),
-            jnp.dot(piece, full_value, preferred_element_type=jnp.float32),
-        ],
-        axis=1,
-    )
+    slab = jnp.concatenate([w_query, key_matrix, value_matrix, w_out.T], axis=1)
+    gathered = weights_of_heads(slab)
+    width = query_cols + 2 * key_cols
+    piece = to_every_tp(normalized_input).reshape(-1, normalized_input.shape[1])
+    joined = jnp.dot(piece, gathered[:, :width], preferred_element_type=jnp.float32)
     raw_q = joined[:, :query_cols]
     raw_k = joined[:, query_cols : query_cols + key_cols]
     raw_v = joined[:, query_cols + key_cols :]
@@ -135,8 +102,13 @@
     vals_now = raw_v.astype(jnp.bfloat16)
     keys_prior, vals_prior = from_behind((keys_now, vals_now), SEQ, 1)
     attended = attend(query_rows, keys_now, vals_now, keys_prior, vals_prior, offset_pos)
-    partial_value = jnp.dot(attended, out_full, preferred_element_type=jnp.float32)
-    own_rows = sum_by_axis(partial_value.astype(jnp.bfloat16), TP, (1, 0), 0).astype(jnp.float32)
+    partial_value = lax.dot_general(
+        attended, gathered[:, width:], (((1,), (1,)), ((), ())), preferred_element_type=jnp.float32
+    )
+    length = lax.axis_size(TP)
+    pieces = partial_value.astype(jnp.bfloat16).reshape(length, -1, partial_value.shape[1])
+    received = lax.all_to_all(pieces, TP, 0, 0, tiled=True)
+    own_rows = jnp.sum(received.astype(jnp.float32), axis=0)
     mixed = root_norm(own_rows, post_gain)
     return (tokens.astype(jnp.float32) + mixed).astype(jnp.bfloat16)
 

time: 358 us -> 191 us (0.53)
  waiting for transfers between devices: 279 us -> 77.1 us
  blocking collectives: 7.6 us -> 51.1 us
  local copies, waits for them, and re-layouts: 7.42 us -> 3.64 us
    reduce_scatter x2 -> x0, waiting for transfers between devices: 83.4 us -> none  [reduced_to_own(): pieces = lax.psum_scatter(pieces, axes[k], scatter_dimension=0, tiled=True)]
    all_gather x2 -> x1, waiting for transfers between devices: 109 us -> 32.5 us  [weights_of_heads(): return lax.all_gather(mine, ('seq_0', 'seq_2'), axis=0, tiled=True)]
    all_to_all x1, waiting for transfers between devices: 84.1 us -> 38.8 us  [to_every_tp(): lax.all_to_all(jnp.broadcast_to(x[None], (length, *x.shape)), TP, 0, 0, t...]
    all_to_all x1, blocking collectives: 7.6 us -> 51.1 us  [local(): received = lax.all_to_all(pieces, TP, 0, 0, tiled=True)]
    all_to_all x1, starting transfers between devices: 16.9 us -> 4.5 us  [to_every_tp(): lax.all_to_all(jnp.broadcast_to(x[None], (length, *x.shape)), TP, 0, 0, t...]
    ppermute x0 -> x2, starting transfers between devices: none -> 10.7 us  [the longest x1 8.75 us: weights_of_heads(): first = lax.ppermute(slab, pair, [(1, 0), (0, 2), (3, 1), (2, 3)])]
    ppermute x0 -> x2, waiting for transfers between devices: none -> 4.78 us  [the longest x1 4.78 us: weights_of_heads(): second = lax.ppermute(slab, pair, [(1, 2), (2, 1)])]
    dot_general x4 -> x2, matrix products: 12 us -> 11.5 us  [the longest x1 7.31 us: local(): jnp.dot(piece, gathered[:, :width], preferred_element_type=jnp.float32)]
  transfers between devices with their start and end apart: 7 -> 6, of which waited for: 5 -> 5; matrix products, arithmetic and copies ran while one was open for 5% -> 5% of each run, Pallas kernels for 0% -> 0%
where the time goes in v1:
time: 191 us
  waiting for transfers between devices  77.1 us (40%)
  blocking collectives  51.1 us (27%)
  starting transfers between devices  20.6 us (11%)
  matrix products  14.6 us (8%)
  between operations  13.6 us (7%)
  other arithmetic  10.2 us (5%)
  local copies, waits for them, and re-layouts  3.64 us (2%)
    all_to_all x1, blocking collectives, local(): received = lax.all_to_all(pieces, TP, 0, 0, tiled=True)  51.1 us
    all_to_all x1, waiting for transfers between devices, to_every_tp(): lax.all_to_all(jnp.broadcast_to(x[None], (length, *x.shape)), TP, 0, 0, t...  38.8 us
    all_gather x1, waiting for transfers between devices, weights_of_heads(): return lax.all_gather(mine, ('seq_0', 'seq_2'), axis=0, tiled=True)  32.5 us
    ppermute x1, starting transfers between devices, weights_of_heads(): first = lax.ppermute(slab, pair, [(1, 0), (0, 2), (3, 1), (2, 3)])  8.75 us
    dot_general x1, matrix products, local(): jnp.dot(piece, gathered[:, :width], preferred_element_type=jnp.float32)  7.31 us
    ppermute x2, starting transfers between devices, from_behind(): return lax.ppermute(x, axis, pairs)  5.39 us
    ppermute x1, waiting for transfers between devices, weights_of_heads(): second = lax.ppermute(slab, pair, [(1, 2), (2, 1)])  4.78 us
    all_to_all x1, starting transfers between devices, to_every_tp(): lax.all_to_all(jnp.broadcast_to(x[None], (length, *x.shape)), TP, 0, 0, t...  4.5 us
  transfers between devices with their start and end apart: 6, of which 5 were waited for; matrix products, arithmetic and copies ran while one was open for 5% of the time, Pallas kernels for 0%

profile of v1, /device:TPU:1, one launch (start us, length us, event | category | flops | bytes accessed | tf_op | source)
XLA Modules:
  0.0 190.8 jit_solution(14534941523644795251)
XLA Ops:
  6.5 0.9 pad_maximum_fusion.1
  7.4 8.7 %collective-permute-start = (bf16[56,1536]{1,0:T(8,128)(2,1)S(1)}, bf16[56,1536]{1,0:T(8,128)(2,1)S(1)}, u32[]{:S(2)}, u32[]{:S(2)}) collective-permute-start(bf16[56,1536]{1,0:T(8,128)(2,1)S(1)} %pad_maximum_fusion.1), channel_id=1, source_target_pairs={{8,0},{0,16},{24,8},{16,24},{9,1},{1,17},{25,9},{17,25},{10,2},{2,... | collective-permute-start | bytes 516104 | tf_op jit(solution)/shard_map/ppermute | solution.py:21
  16.2 1.9 %collective-permute-start.1 = (bf16[56,1536]{1,0:T(8,128)(2,1)S(1)}, bf16[56,1536]{1,0:T(8,128)(2,1)S(1)}, u32[]{:S(2)}, u32[]{:S(2)}) collective-permute-start(bf16[56,1536]{1,0:T(8,128)(2,1)S(1)} %pad_maximum_fusion.1), channel_id=1, source_target_pairs={{8,16},{16,8},{9,17},{17,9},{10,18},{18,10},{11,19},{19,11},{12,20... | collective-permute-start | bytes 516104 | tf_op jit(solution)/shard_map/ppermute | solution.py:22
  18.1 4.8 %collective-permute-done.1 = bf16[56,1536]{1,0:T(8,128)(2,1)S(1)} collective-permute-done((bf16[56,1536]{1,0:T(8,128)(2,1)S(1)}, bf16[56,1536]{1,0:T(8,128)(2,1)S(1)}, u32[]{:S(2)}, u32[]{:S(2)}) %collective-permute-start.1) | collective-permute-done | bytes 172064 | tf_op jit(solution)/shard_map/ppermute | solution.py:22
  22.9 1.0 select_select_fusion.1
  23.9 0.8 pad_maximum_fusion
  24.7 1.2 fusion.18
  25.9 1.2 fusion.20
  27.1 2.1 %broadcast_in_dim.8 = bf16[8,64,3584]{2,1,0:T(8,128)(2,1)} broadcast(bf16[64,3584]{1,0:T(8,128)(2,1)S(1)} %fusion.20), dimensions={1,2} | broadcast | bytes 4128768 | tf_op jit(solution)/shard_map/broadcast_in_dim | solution.py:16
  29.2 4.5 %all-to-all-start = ((bf16[8,64,3584]{2,1,0:T(8,128)(2,1)}), bf16[8,64,3584]{2,1,0:T(8,128)(2,1)}, u32[]{:S(2)}, u32[]{:S(2)}) async-start(bf16[8,64,3584]{2,1,0:T(8,128)(2,1)} %broadcast_in_dim.8), calls=%async_computation | async-start | bytes 7340032 | tf_op jit(solution)/shard_map/all_to_all | solution.py:16
  33.8 1.0 multiply_cosine_fusion
  35.2 38.8 %all-to-all-done = bf16[8,64,3584]{2,1,0:T(8,128)(2,1)} async-done(((bf16[8,64,3584]{2,1,0:T(8,128)(2,1)}), bf16[8,64,3584]{2,1,0:T(8,128)(2,1)}, u32[]{:S(2)}, u32[]{:S(2)}) %all-to-all-start) | async-done | bytes 3670048 | tf_op jit(solution)/shard_map/all_to_all | solution.py:16
  74.0 32.5 %all-gather.2.cloned.1.call-done = bf16[3584,1536]{1,0:T(8,128)(2,1)} async-done(((bf16[112,1536]{1,0:T(8,128)(2,1)}), bf16[3584,1536]{1,0:T(8,128)(2,1)}) %all-gather.2.cloned.1.call-update) | async-done | bytes 11010064 | tf_op jit(solution)/shard_map/all_gather | solution.py:28
  106.6 7.3 %fusion = f32[512,1024]{1,0:T(8,128)S(1)} fusion(bf16[512,3584]{1,0:T(8,128)(2,1)} %bitcast, bf16[3584,1536]{1,0:T(8,128)(2,1)} %all-gather.2.cloned.1.call-done), kind=kOutput, calls=%fused_computation | convolution fusion | flops 3758096384 | bytes 13107200 | tf_op jit(solution)/shard_map/dot_general | solution.py:94
  114.1 1.2 fusion.34
  115.3 0.7 maximum_bitcast_fusion.4
  116.0 3.2 %collective-permute-start.3 = (bf16[512,256]{1,0:T(8,128)(2,1)}, bf16[512,256]{1,0:T(8,128)(2,1)}, u32[]{:S(2)}, u32[]{:S(2)}) collective-permute-start(bf16[512,256]{1,0:T(8,128)(2,1)} %maximum_bitcast_fusion.4), channel_id=1, source_target_pairs={{0,8},{8,16},{16,24},{24,32},{32,40},{40,48},{48,56},{56,64},{64,7... | collective-permute-start | bytes 786440 | tf_op jit(solution)/shard_map/ppermute | solution.py:34
  120.3 2.1 %collective-permute-start.2 = (bf16[512,256]{1,0:T(8,128)(2,1)S(1)}, bf16[512,256]{1,0:T(8,128)(2,1)S(1)}, u32[]{:S(2)}, u32[]{:S(2)}) collective-permute-start(bf16[512,256]{1,0:T(8,128)(2,1)S(1)} %slice.56), channel_id=1, source_target_pairs={{0,8},{8,16},{16,24},{24,32},{32,40},{40,48},{48,56},{56,64},{64,7... | collective-permute-start | bytes 786440 | tf_op jit(solution)/shard_map/ppermute | solution.py:34
  122.9 2.1 %fusion.2 = (f32[2,512]{1,0:T(2,128)S(1)}, f32[1024,512,2]{1,0,2:T(8,128)S(1)}) fusion(pred[512,1024]{0,1:T(8,128)(4,1)S(1)} %fusion.10, f32[512,2,128]{2,0,1:T(8,128)S(1)} %get-tuple-element.6, f32[512,2,128]{2,0,1:T(8,128)S(1)} %get-tuple-element.5, bf16[512,256]{1,0:T(8,128)(2,1)} %maximum_bitcast_fusion.4, bf16[512,256]{1,0:T(8,128)(2,1)} %collective-permute-done.3), kind=kOutput, calls=%fused_computation.5 | convolution fusion | flops 540802048 | bytes 6295552 | tf_op jit(solution)/shard_map/cwap,bwp->wacb/dot_general | solution.py:69
  125.0 0.8 collective-permute-done.2
  125.8 1.0 divide_convert_fusion
  126.8 4.2 %convolution_convert_fusion = bf16[512,3584]{1,0:T(8,128)(2,1)S(1)} fusion(bf16[512,512]{0,1:T(8,128)(2,1)S(1)} %bitcast.54, bf16[3584,1536]{1,0:T(8,128)(2,1)} %all-gather.2.cloned.1.call-done), kind=kOutput, calls=%fused_computation.3 | convolution fusion | flops 1880883200 | bytes 7864320 | tf_op jit(solution)/shard_map/dot_general | solution.py:105
  131.0 51.1 %all_to_all.10 = bf16[8,64,3584]{2,1,0:T(8,128)(2,1)S(1)} all-to-all(bf16[8,64,3584]{2,1,0:T(8,128)(2,1)S(1)} %bitcast.51), channel_id=1, replica_groups=mesh['seq_0'=16,'seq_1'=2,'seq_2'=2,'tp_0'=2,'tp_1'=4] {'tp_0','tp_1'}, dimensions={0} | all-to-all | bytes 7340032 | tf_op jit(solution)/shard_map/all_to_all | solution.py:110
  183.0 1.0 fusion.21
  (23 shorter events, 3.1 us)
Async XLA Ops:
  6.5 100.0 %all-gather.2.cloned.1.call-start = ((), (), s32[]{:S(2)}) async-start(), calls=%async_computation.2 | async-start | bytes 11354112 | tf_op jit(solution)/shard_map/all_gather | solution.py:28
  7.4 10.7 %collective-permute-start = (bf16[56,1536]{1,0:T(8,128)(2,1)S(1)}, bf16[56,1536]{1,0:T(8,128)(2,1)S(1)}, u32[]{:S(2)}, u32[]{:S(2)}) collective-permute-start(bf16[56,1536]{1,0:T(8,128)(2,1)S(1)} %pad_maximum_fusion.1), channel_id=1, source_target_pairs={{8,0},{0,16},{24,8},{16,24},{9,1},{1,17},{25,9},{17,25},{10,2},{2,... | collective-permute-start | bytes 516104 | tf_op jit(solution)/shard_map/ppermute | solution.py:21
  16.2 6.7 %collective-permute-start.1 = (bf16[56,1536]{1,0:T(8,128)(2,1)S(1)}, bf16[56,1536]{1,0:T(8,128)(2,1)S(1)}, u32[]{:S(2)}, u32[]{:S(2)}) collective-permute-start(bf16[56,1536]{1,0:T(8,128)(2,1)S(1)} %pad_maximum_fusion.1), channel_id=1, source_target_pairs={{8,16},{16,8},{9,17},{17,9},{10,18},{18,10},{11,19},{19,11},{12,20... | collective-permute-start | bytes 516104 | tf_op jit(solution)/shard_map/ppermute | solution.py:22
  29.2 44.8 %all-to-all-start = ((bf16[8,64,3584]{2,1,0:T(8,128)(2,1)}), bf16[8,64,3584]{2,1,0:T(8,128)(2,1)}, u32[]{:S(2)}, u32[]{:S(2)}) async-start(bf16[8,64,3584]{2,1,0:T(8,128)(2,1)} %broadcast_in_dim.8), calls=%async_computation | async-start | bytes 7340032 | tf_op jit(solution)/shard_map/all_to_all | solution.py:16
  116.0 6.9 %collective-permute-start.3 = (bf16[512,256]{1,0:T(8,128)(2,1)}, bf16[512,256]{1,0:T(8,128)(2,1)}, u32[]{:S(2)}, u32[]{:S(2)}) collective-permute-start(bf16[512,256]{1,0:T(8,128)(2,1)} %maximum_bitcast_fusion.4), channel_id=1, source_target_pairs={{0,8},{8,16},{16,24},{24,32},{32,40},{40,48},{48,56},{56,64},{64,7... | collective-permute-start | bytes 786440 | tf_op jit(solution)/shard_map/ppermute | solution.py:34
  120.3 5.4 %collective-permute-start.2 = (bf16[512,256]{1,0:T(8,128)(2,1)S(1)}, bf16[512,256]{1,0:T(8,128)(2,1)S(1)}, u32[]{:S(2)}, u32[]{:S(2)}) collective-permute-start(bf16[512,256]{1,0:T(8,128)(2,1)S(1)} %slice.56), channel_id=1, source_target_pairs={{0,8},{8,16},{16,24},{24,32},{32,40},{40,48},{48,56},{56,64},{64,7... | collective-permute-start | bytes 786440 | tf_op jit(solution)/shard_map/ppermute | solution.py:34
  182.0 1.0 copy-start
  182.0 1.0 copy-start.1
Sparse Core Ops, SparseCore 0:
  24.8 81.6 all-gather.1

commit v2 on v1

v2 whole, which is shorter than its diff:
```python
import jax
import jax.numpy as jnp
from jax import lax
from jax.experimental import pallas as pl
from jax.experimental.pallas import tpu as pltpu
from jax.sharding import Mesh
from jax.sharding import PartitionSpec as P

HEAD_SIZE = 256
BLOCK_TOKENS = 512
SEQ = ("seq_0", "seq_1", "seq_2")
TP = ("tp_0", "tp_1")
SEQ_TP = ("seq_0", "seq_1", "seq_2", "tp_0", "tp_1")


def to_every_tp(x):
    length = lax.axis_size(TP)
    return lax.all_to_all(jnp.broadcast_to(x[None], (length, *x.shape)), TP, 0, 0, tiled=True)


def weights_of_heads(slab):
    beside = lax.ppermute(slab, "seq_1", [(0, 1), (1, 0)])
    first = lax.axis_index("seq_1") == 0
    both = jnp.concatenate([jnp.where(first, slab, beside), jnp.where(first, beside, slab)], axis=0)
    gathered = lax.all_gather(both, ("seq_0", "seq_2"), axis=0, tiled=True)
    return gathered.reshape(lax.axis_size("seq_0"), 2, 2, *slab.shape)


def from_behind(x, axis, by):
    length = lax.axis_size(axis)
    pairs = [(i, i + by) for i in range(length) if 0 <= i + by < length]
    return lax.ppermute(x, axis, pairs)


def root_norm(values, gain):
    values = values.astype(jnp.float32)
    return values * lax.rsqrt(jnp.mean(values * values, axis=-1, keepdims=True) + 1e-06) * gain


CHUNKS = 4


def angles(token_positions):
    half_dim = HEAD_SIZE // 2
    freq = 10000.0 ** (-(jnp.arange(half_dim).astype(jnp.float32) * 2.0 / HEAD_SIZE))
    angle = token_positions[:, None] * freq[None, :]
    return jnp.cos(angle), jnp.sin(angle)


def weight_copies(w_hbm, w_vmem, sems, column, depths):
    rows, width = w_hbm.shape[3], w_vmem.shape[1]
    each = depths // CHUNKS
    copies = []
    for chunk in range(CHUNKS):
        for z in range(chunk * each, (chunk + 1) * each):
            for core in range(2):
                for chip in range(2):
                    at = ((z * 2 + chip) * 2 + core) * rows
                    copies.append(
                        pltpu.make_async_copy(
                            w_hbm.at[z, core, chip, :, pl.ds(column, width)],
                            w_vmem.at[pl.ds(at, rows), :],
                            sems.at[len(copies)],
                        )
                    )
    return copies


def turned(values, cosine, sine):
    half = HEAD_SIZE // 2
    first, second = values[:, :half], values[:, half:]
    return jnp.concatenate([first * cosine - second * sine, second * cosine + first * sine], axis=1)


def projected(x_hbm, w_hbm, x_vmem, w_vmem, x_sems, w_sems, column):
    copies = weight_copies(w_hbm, w_vmem, w_sems, column, w_hbm.shape[0])
    per = len(copies) // CHUNKS
    depth = x_vmem.shape[1] // CHUNKS
    x_copies = [
        pltpu.make_async_copy(
            x_hbm.at[:, pl.ds(k * depth, depth)], x_vmem.at[:, pl.ds(k * depth, depth)], x_sems.at[k]
        )
        for k in range(CHUNKS)
    ]
    for k in range(CHUNKS):
        x_copies[k].start()
        for copy in copies[k * per : (k + 1) * per]:
            copy.start()
    total = None
    for k in range(CHUNKS):
        x_copies[k].wait()
        for copy in copies[k * per : (k + 1) * per]:
            copy.wait()
        part = jnp.dot(
            x_vmem[:, k * depth : (k + 1) * depth],
            w_vmem[k * depth : (k + 1) * depth, :],
            preferred_element_type=jnp.float32,
        )
        total = part if total is None else total + part
    return total


def kv_kernel(x_hbm, w_hbm, cos_ref, sin_ref, out_ref, x_vmem, w_vmem, x_sems, w_sems, *, column):
    total = projected(x_hbm, w_hbm, x_vmem, w_vmem, x_sems, w_sems, column)
    out_ref[:, :HEAD_SIZE] = turned(total[:, :HEAD_SIZE], cos_ref[...], sin_ref[...]).astype(jnp.bfloat16)
    out_ref[:, HEAD_SIZE:] = total[:, HEAD_SIZE:].astype(jnp.bfloat16)


def q_kernel(x_hbm, w_hbm, cos_ref, sin_ref, out_ref, x_vmem, w_vmem, x_sems, w_sems, *, column):
    total = projected(x_hbm, w_hbm, x_vmem, w_vmem, x_sems, w_sems, column)
    for head in range(total.shape[1] // HEAD_SIZE):
        part = slice(head * HEAD_SIZE, (head + 1) * HEAD_SIZE)
        rotated = turned(total[:, part], cos_ref[...], sin_ref[...])
        out_ref[:, part] = (rotated * HEAD_SIZE ** (-0.5)).astype(jnp.bfloat16)


def projection(kernel, piece, gathered, cosine, sine, column, width):
    rows, depth = piece.shape
    copies = gathered.shape[0] * 4
    anywhere, inside = pl.BlockSpec(memory_space=pl.ANY), pl.BlockSpec(memory_space=pltpu.VMEM)
    return pl.pallas_call(
        lambda *refs: kernel(*refs, column=column),
        out_shape=jax.ShapeDtypeStruct((rows, width), jnp.bfloat16),
        in_specs=[anywhere, anywhere, inside, inside],
        out_specs=inside,
        scratch_shapes=[
            pltpu.VMEM((rows, depth), jnp.bfloat16),
            pltpu.VMEM((depth, width), jnp.bfloat16),
            pltpu.SemaphoreType.DMA((CHUNKS,)),
            pltpu.SemaphoreType.DMA((copies,)),
        ],
        cost_estimate=pl.CostEstimate(
            flops=2 * rows * depth * width, transcendentals=0, bytes_accessed=2 * depth * (rows + width)
        ),
        name=kernel.__name__,
    )(piece, gathered, cosine, sine)


TILE = 128


def attend_kernel(least_ref, q_ref, now_ref, prior_ref, w_hbm, out_hbm, keys, held, w_vmem, made, w_sems, out_sems, *, column):
    copies = weight_copies(w_hbm, w_vmem, w_sems, column, w_hbm.shape[0])
    for copy in copies:
        copy.start()
    length = q_ref.shape[0]
    heads = q_ref.shape[1] // HEAD_SIZE
    keys[:length, :] = prior_ref[...]
    keys[length:, :] = now_ref[...]
    span = length + TILE
    row = lax.broadcasted_iota(jnp.int32, (heads, TILE, span), 1).reshape(heads * TILE, span)
    column_at = lax.broadcasted_iota(jnp.int32, (heads * TILE, span), 1)
    window = (column_at > row) & (column_at <= row + length)
    for t in range(length // TILE):
        at = t * TILE
        q = jnp.concatenate(
            [q_ref[at : at + TILE, h * HEAD_SIZE : (h + 1) * HEAD_SIZE] for h in range(heads)], axis=0
        )
        scores = lax.dot_general(
            q, keys[at : at + span, :HEAD_SIZE], (((1,), (1,)), ((), ())), preferred_element_type=jnp.float32
        )
        seen = window & (column_at + at >= least_ref[0])
        weights = jnp.where(seen, jnp.exp(scores), 0.0)
        denom = jnp.sum(weights, axis=1, keepdims=True)
        reduced = jnp.dot(
            weights.astype(jnp.bfloat16), keys[at : at + span, HEAD_SIZE:], preferred_element_type=jnp.float32
        )
        reduced = (reduced / denom).astype(jnp.bfloat16)
        for h in range(heads):
            held[at : at + TILE, h * HEAD_SIZE : (h + 1) * HEAD_SIZE] = reduced[h * TILE : (h + 1) * TILE]
    per = len(copies) // CHUNKS
    width = w_vmem.shape[0] // CHUNKS
    sends = []
    for k in range(CHUNKS):
        for copy in copies[k * per : (k + 1) * per]:
            copy.wait()
        part = pl.ds(k * width, width)
        made[:, part] = lax.dot_general(
            held[...], w_vmem[part, :], (((1,), (1,)), ((), ())), preferred_element_type=jnp.float32
        ).astype(jnp.bfloat16)
        sends.append(pltpu.make_async_copy(made.at[:, part], out_hbm.at[:, part], out_sems.at[k]))
        sends[-1].start()
    for send in sends:
        send.wait()


def attended_out(queries, now, prior, gathered, least, column):
    length, width = queries.shape
    depth = gathered.shape[0] * 4 * gathered.shape[3]
    anywhere, inside = pl.BlockSpec(memory_space=pl.ANY), pl.BlockSpec(memory_space=pltpu.VMEM)
    return pl.pallas_call(
        lambda *refs: attend_kernel(*refs, column=column),
        out_shape=jax.ShapeDtypeStruct((length, depth), jnp.bfloat16),
        in_specs=[pl.BlockSpec(memory_space=pltpu.SMEM), inside, inside, inside, anywhere],
        out_specs=anywhere,
        scratch_shapes=[
            pltpu.VMEM((2 * length, 2 * HEAD_SIZE), jnp.bfloat16),
            pltpu.VMEM((length, width), jnp.bfloat16),
            pltpu.VMEM((depth, width), jnp.bfloat16),
            pltpu.VMEM((length, depth), jnp.bfloat16),
            pltpu.SemaphoreType.DMA((gathered.shape[0] * 4,)),
            pltpu.SemaphoreType.DMA((CHUNKS,)),
        ],
        cost_estimate=pl.CostEstimate(
            flops=2 * length * width * (depth + 4 * length), transcendentals=2 * length * length, bytes_accessed=4 * depth * width
        ),
        name="attend_kernel",
    )(least, queries, now, prior, gathered)


def local(tokens, pre_gain, post_gain, w_query, key_matrix, value_matrix, w_out):
    normalized_input = root_norm(tokens, pre_gain).astype(jnp.bfloat16)
    query_cols = w_query.shape[1]
    key_cols = key_matrix.shape[1]
    slab = jnp.concatenate([w_query, key_matrix, value_matrix, w_out.T], axis=1)
    gathered = weights_of_heads(slab)
    width = query_cols + 2 * key_cols
    piece = to_every_tp(normalized_input).reshape(-1, normalized_input.shape[1])
    offset_pos = lax.axis_index(SEQ) * BLOCK_TOKENS
    cosine, sine = angles((offset_pos + jnp.arange(BLOCK_TOKENS)).astype(jnp.float32))
    now = projection(kv_kernel, piece, gathered, cosine, sine, query_cols, 2 * key_cols)
    prior = from_behind(now, SEQ, 1)
    queries = projection(q_kernel, piece, gathered, cosine, sine, 0, query_cols)
    least = jnp.where(offset_pos > 0, 0, BLOCK_TOKENS).astype(jnp.int32).reshape(1)
    partial_value = attended_out(queries, now, prior, gathered, least, width)
    length = lax.axis_size(TP)
    pieces = partial_value.reshape(length, -1, partial_value.shape[1])
    received = lax.all_to_all(pieces, TP, 0, 0, tiled=True)
    own_rows = jnp.sum(received.astype(jnp.float32), axis=0)
    mixed = root_norm(own_rows, post_gain)
    return (tokens.astype(jnp.float32) + mixed).astype(jnp.bfloat16)


def solution(mesh):
    finer = Mesh(mesh.devices.reshape(16, 2, 2, 2, 4), ("seq_0", "seq_1", "seq_2", "tp_0", "tp_1"))
    in_specs = (P(SEQ_TP, None), P(), P(), P(SEQ, TP), P(SEQ, TP), P(SEQ, TP), P(TP, SEQ))
    out_specs = P(SEQ_TP, None)
    return jax.shard_map(local, mesh=finer, in_specs=in_specs, out_specs=out_specs, check_vma=False)
```

time: 191 us -> 193 us (1.010)
  Pallas kernels: 0 us -> 22.5 us
  matrix products: 14.6 us -> 0 us
  starting transfers between devices: 20.6 us -> 15.1 us
    pallas_call x0 -> x3, Pallas kernels: none -> 22.5 us  [the longest x2 15.3 us: projection(): pl.pallas_call(lambda *refs: kernel(*refs, column=column), out_shape=jax....]
    dot_general x4 -> x0, matrix products: 14.6 us -> none  [the longest x1 7.31 us: local(): jnp.dot(piece, gathered[:, :width], preferred_element_type=jnp.float32)]
    ppermute x2 -> x1, starting transfers between devices: 10.7 us -> 3.94 us  [weights_of_heads(): beside = lax.ppermute(slab, 'seq_1', [(0, 1), (1, 0)])]
    all_to_all x1, starting transfers between devices: 4.5 us -> 7.9 us  [to_every_tp(): lax.all_to_all(jnp.broadcast_to(x[None], (length, *x.shape)), TP, 0, 0, t...]
    all_to_all x1, waiting for transfers between devices: 38.8 us -> 41.3 us  [to_every_tp(): lax.all_to_all(jnp.broadcast_to(x[None], (length, *x.shape)), TP, 0, 0, t...]
    ppermute x2 -> x1, starting transfers between devices: 5.39 us -> 3.26 us  [from_behind(): return lax.ppermute(x, axis, pairs)]
    ppermute x2 -> x1, waiting for transfers between devices: 4.78 us -> 2.77 us  [weights_of_heads(): beside = lax.ppermute(slab, 'seq_1', [(0, 1), (1, 0)])]
  transfers between devices with their start and end apart: 6 -> 4, of which waited for: 5 -> 3; matrix products, arithmetic and copies ran while one was open for 5% -> 3% of each run, Pallas kernels for 0% -> 4%
where the time goes in v2:
time: 193 us; the launch traced here: 192 us
  waiting for transfers between devices  78.3 us (41%)
  blocking collectives  51.1 us (26%)
  Pallas kernels  22.5 us (12%)
  starting transfers between devices  15.1 us (8%)
  between operations  13.5 us (7%)
  other arithmetic  8.48 us (4%)
  local copies, waits for them, and re-layouts  3.23 us (2%)
    all_to_all x1, blocking collectives, local(): received = lax.all_to_all(pieces, TP, 0, 0, tiled=True)  51.1 us
    all_to_all x1, waiting for transfers between devices, to_every_tp(): lax.all_to_all(jnp.broadcast_to(x[None], (length, *x.shape)), TP, 0, 0, t...  41.3 us
    all_gather x1, waiting for transfers between devices, weights_of_heads(): gathered = lax.all_gather(both, ('seq_0', 'seq_2'), axis=0, tiled=True)  34.1 us
    pallas_call x2, Pallas kernels, projection(): pl.pallas_call(lambda *refs: kernel(*refs, column=column), out_shape=jax....  15.3 us
    all_to_all x1, starting transfers between devices, to_every_tp(): lax.all_to_all(jnp.broadcast_to(x[None], (length, *x.shape)), TP, 0, 0, t...  7.9 us
    pallas_call x1, Pallas kernels, attended_out(): pl.pallas_call(lambda *refs: attend_kernel(*refs, column=column), out_sha...  7.22 us
    ppermute x1, starting transfers between devices, weights_of_heads(): beside = lax.ppermute(slab, 'seq_1', [(0, 1), (1, 0)])  3.94 us
  transfers between devices with their start and end apart: 4, of which 3 were waited for; matrix products, arithmetic and copies ran while one was open for 3% of the time, Pallas kernels for 4%

profile of v2, /device:TPU:1, one launch (start us, length us, event | category | flops | bytes accessed | tf_op | source)
XLA Modules:
  0.0 192.2 jit_solution(7290402305032560951)
XLA Ops:
  6.5 0.9 pad_maximum_fusion.1
  7.4 3.9 %collective-permute-start = (bf16[56,1536]{1,0:T(8,128)(2,1)S(1)}, bf16[56,1536]{1,0:T(8,128)(2,1)S(1)}, u32[]{:S(2)}, u32[]{:S(2)}) collective-permute-start(bf16[56,1536]{1,0:T(8,128)(2,1)S(1)} %pad_maximum_fusion.1), channel_id=1, source_target_pairs={{0,16},{16,0},{1,17},{17,1},{2,18},{18,2},{3,19},{19,3},{4,20},{20... | collective-permute-start | bytes 516104 | tf_op jit(solution)/shard_map/ppermute | solution.py:22
  11.4 2.8 %collective-permute-done = bf16[56,1536]{1,0:T(8,128)(2,1)S(1)} collective-permute-done((bf16[56,1536]{1,0:T(8,128)(2,1)S(1)}, bf16[56,1536]{1,0:T(8,128)(2,1)S(1)}, u32[]{:S(2)}, u32[]{:S(2)}) %collective-permute-start) | collective-permute-done | bytes 172064 | tf_op jit(solution)/shard_map/ppermute | solution.py:22
  14.2 0.9 broadcast_select_fusion.1
  15.1 0.8 pad_maximum_fusion
  15.9 0.0 all-gather.2.cloned.1.call-update
  15.9 1.2 fusion
  17.1 1.2 fusion.2
  18.3 2.1 %broadcast_in_dim.2 = bf16[8,64,3584]{2,1,0:T(8,128)(2,1)} broadcast(bf16[64,3584]{1,0:T(8,128)(2,1)S(1)} %fusion.2), dimensions={1,2} | broadcast | bytes 4128768 | tf_op jit(solution)/shard_map/broadcast_in_dim | solution.py:18
  20.4 7.9 %all-to-all-start = ((bf16[8,64,3584]{2,1,0:T(8,128)(2,1)}), bf16[8,64,3584]{2,1,0:T(8,128)(2,1)}, u32[]{:S(2)}, u32[]{:S(2)}) async-start(bf16[8,64,3584]{2,1,0:T(8,128)(2,1)} %broadcast_in_dim.2), calls=%async_computation | async-start | bytes 7340032 | tf_op jit(solution)/shard_map/all_to_all | solution.py:18
  28.3 1.8 multiply_sine_fusion
  30.2 41.3 %all-to-all-done = bf16[8,64,3584]{2,1,0:T(8,128)(2,1)} async-done(((bf16[8,64,3584]{2,1,0:T(8,128)(2,1)}), bf16[8,64,3584]{2,1,0:T(8,128)(2,1)}, u32[]{:S(2)}, u32[]{:S(2)}) %all-to-all-start) | async-done | bytes 3670048 | tf_op jit(solution)/shard_map/all_to_all | solution.py:18
  71.5 34.1 %all-gather.2.cloned.1.call-done = bf16[3584,1536]{1,0:T(8,128)(2,1)} async-done(((bf16[112,1536]{1,0:T(8,128)(2,1)}), bf16[3584,1536]{1,0:T(8,128)(2,1)}) %all-gather.2.cloned.1.call-update) | async-done | bytes 11010064 | tf_op jit(solution)/shard_map/all_gather | solution.py:25
  105.6 7.6 %kv_kernel.1.refs_2_ = bf16[512,512]{1,0:T(8,128)(2,1)} custom-call(bf16[512,3584]{1,0:T(8,128)(2,1)} %bitcast.1.refs_0_, bf16[16,2,2,56,1536]{4,3,2,1,0:T(8,128)(2,1)} %bitcast.5, f32[512,128]{1,0:T(8,128)} %get-tuple-element.8.refs_2_, f32[512,128]{1,0:T(8,128)} %get-tuple-element.7.refs_3_), custom_call_target="tpu_custom_call" | custom-call | flops 1879048192 | bytes 7340032 | tf_op jit(solution)/shard_map/kv_kernel/pallas_call | solution.py:121
  113.3 3.3 %collective-permute-start.1 = (bf16[512,512]{1,0:T(8,128)(2,1)}, bf16[512,512]{1,0:T(8,128)(2,1)S(1)}, u32[]{:S(2)}, u32[]{:S(2)}) collective-permute-start(bf16[512,512]{1,0:T(8,128)(2,1)} %kv_kernel.1.refs_2_), channel_id=1, source_target_pairs={{0,8},{8,16},{16,24},{24,32},{32,40},{40,48},{48,56},{56,64},{64,7... | collective-permute-start | bytes 1572872 | tf_op jit(solution)/shard_map/ppermute | solution.py:32
  116.5 7.6 %q_kernel.1.refs_1_ = bf16[512,512]{1,0:T(8,128)(2,1)} custom-call(bf16[512,3584]{1,0:T(8,128)(2,1)} %bitcast.1.refs_0_, bf16[16,2,2,56,1536]{4,3,2,1,0:T(8,128)(2,1)} %bitcast.6, f32[512,128]{1,0:T(8,128)} %get-tuple-element.8.refs_2_, f32[512,128]{1,0:T(8,128)} %get-tuple-element.7.refs_3_), custom_call_target="tpu_custom_call" | custom-call | flops 1879048192 | bytes 7340032 | tf_op jit(solution)/shard_map/q_kernel/pallas_call | solution.py:121
  124.2 0.0 collective-permute-done.1.refs_3_
  124.2 0.8 copy-done.1
  125.0 7.2 %attend_kernel.1 = bf16[512,3584]{1,0:T(8,128)(2,1)} custom-call(s32[1]{0:T(128)} %bitcast.refs_0_, bf16[512,512]{1,0:T(8,128)(2,1)} %q_kernel.1.refs_1_, bf16[512,512]{1,0:T(8,128)(2,1)} %kv_kernel.1.refs_2_, bf16[512,512]{1,0:T(8,128)(2,1)} %copy-done.1, bf16[16,2,2,56,1536]{4,3,2,1,0:T(8,128)(2,1)} %bitcast.7), custom_call_target="tpu_custom_call" | custom-call | flops 2952790016 | bytes 7340032 | tf_op jit(solution)/shard_map/attend_kernel/pallas_call | solution.py:191
  132.2 51.1 %all_to_all.10 = bf16[8,64,3584]{2,1,0:T(8,128)(2,1)S(1)} all-to-all(bf16[8,64,3584]{2,1,0:T(8,128)(2,1)} %bitcast.8), channel_id=1, replica_groups=mesh['seq_0'=16,'seq_1'=2,'seq_2'=2,'tp_0'=2,'tp_1'=4] {'tp_0','tp_1'}, dimensions={0} | all-to-all | bytes 7340032 | tf_op jit(solution)/shard_map/all_to_all | solution.py:228
  183.3 0.5 convert_reduce_fusion
  183.8 0.2 multiply_reduce_fusion
  184.0 0.3 copy-done
  184.3 1.0 fusion.3
  (9 shorter events, 0.0 us)
Async XLA Ops:
  6.5 99.1 %all-gather.2.cloned.1.call-start = ((), (), s32[]{:S(2)}) async-start(), calls=%async_computation.2 | async-start | bytes 11354112 | tf_op jit(solution)/shard_map/all_gather | solution.py:25
  7.4 6.7 %collective-permute-start = (bf16[56,1536]{1,0:T(8,128)(2,1)S(1)}, bf16[56,1536]{1,0:T(8,128)(2,1)S(1)}, u32[]{:S(2)}, u32[]{:S(2)}) collective-permute-start(bf16[56,1536]{1,0:T(8,128)(2,1)S(1)} %pad_maximum_fusion.1), channel_id=1, source_target_pairs={{0,16},{16,0},{1,17},{17,1},{2,18},{18,2},{3,19},{19,3},{4,20},{20... | collective-permute-start | bytes 516104 | tf_op jit(solution)/shard_map/ppermute | solution.py:22
  20.4 51.1 %all-to-all-start = ((bf16[8,64,3584]{2,1,0:T(8,128)(2,1)}), bf16[8,64,3584]{2,1,0:T(8,128)(2,1)}, u32[]{:S(2)}, u32[]{:S(2)}) async-start(bf16[8,64,3584]{2,1,0:T(8,128)(2,1)} %broadcast_in_dim.2), calls=%async_computation | async-start | bytes 7340032 | tf_op jit(solution)/shard_map/all_to_all | solution.py:18
  113.3 10.9 %collective-permute-start.1 = (bf16[512,512]{1,0:T(8,128)(2,1)}, bf16[512,512]{1,0:T(8,128)(2,1)S(1)}, u32[]{:S(2)}, u32[]{:S(2)}) collective-permute-start(bf16[512,512]{1,0:T(8,128)(2,1)} %kv_kernel.1.refs_2_), channel_id=1, source_target_pairs={{0,8},{8,16},{16,24},{24,32},{32,40},{40,48},{48,56},{56,64},{64,7... | collective-permute-start | bytes 1572872 | tf_op jit(solution)/shard_map/ppermute | solution.py:32
  124.2 0.8 copy-start.1
  183.3 1.0 copy-start
  183.3 1.0 copy-start.2
Sparse Core Ops, SparseCore 0:
  16.0 89.5 all-gather.1
